TPU v7x, 32 devices: a whole 2x2x4 slice. The times are simulated.
32 devices in a mesh: seq: 2 (over core), mp: 4 (over y, x), batch: 4 (over z).
Axes of the slice: x: 2, y: 2, z: 4, core: 2. Of those that a mesh axis runs over, the one named last changes fastest.
Arguments:
- queries: bfloat16 [4, 8, 4096], P('batch', 'seq', 'mp'), may hold values from -6 to 6
- keys: bfloat16 [4, 512, 1024], P('batch', 'seq', 'mp'), may hold values from -6 to 6
- values: bfloat16 [4, 512, 1024], P('batch', 'seq', 'mp'), may hold values from -6 to 6
- key_position: float32 [32, 128], replicated, may hold values from -4 to 4
- compress_keys: bfloat16 [4096, 128], replicated, may hold values from -0.2 to 0.2
- compress_values: bfloat16 [4096, 128], replicated, may hold values from -0.09375 to 0.09375
- out_proj: bfloat16 [4096, 4096], P('mp', 'seq'), may hold values from -0.09375 to 0.09375
- residual: bfloat16 [4, 8, 4096], P(None, None, 'seq'), may hold values from -6 to 6
- norm_gain: float32 [4096], replicated, may hold values from 0.25 to 1.75
- lm_head: bfloat16 [8192, 4096], P(('seq', 'mp', 'batch')), may hold values from -0.4 to 0.4
- targets: int32 [4, 8], replicated, may hold values from 0 to 8191
- lengths: int32 [4], replicated, may hold values from 128 to 512
Outputs:
- token_logprob: float32 [4, 8], P('batch', 'seq')
- rollout_score: float32 [4], P('batch')
All inputs are finite; a program needn't handle non-finite values.
Results may differ from a plain program's by a relative error of at most 0.0005.
The roundings to bfloat16 on the way count: a program that leaves them out, or rounds other values in their place, can miss the bound.
Values may be sent and summed in bfloat16 or wider, within the bound.
No kernel may reach another device: no remote copies, remote signals or barrier semaphores. Data moves between devices by JAX's collectives and lax.ppermute only.
A program may use at most 64 MiB of HBM per device.

v0:
```python
import math
import jax
import jax.numpy as jnp
from jax import lax
from jax.sharding import PartitionSpec as P

HEAD_DIM = 128
BLOCK = 32
STRIDE = 16


def from_behind(block, axis, distance):
    devices = range(lax.axis_size(axis))
    route = [(i - distance, i) for i in devices if i - distance in devices]
    return lax.ppermute(block, axis, route)


def compress_rows(rows, following, position, weight):
    extended = jnp.concatenate([rows, following], 0)
    count = rows.shape[0] // STRIDE
    heads = rows.shape[1] // HEAD_DIM
    shaped = extended.reshape(count + 1, STRIDE, heads, HEAD_DIM)
    blocks = jnp.concatenate([shaped[:-1], shaped[1:]], 1)
    blocks = (blocks.astype(jnp.float32) + position[None, :, None, :]).astype(jnp.bfloat16)
    mapped = jnp.einsum(
        "bjhd,jde->bhe",
        blocks,
        weight.reshape(BLOCK, HEAD_DIM, HEAD_DIM),
        preferred_element_type=jnp.float32,
    )
    return mapped.astype(jnp.bfloat16).reshape(count, heads * HEAD_DIM)


def normalize(hidden, gain):
    widened = hidden.astype(jnp.float32)
    meansq = jnp.mean(widened * widened, -1, keepdims=True)
    return (widened * lax.rsqrt(meansq + 1e-05) * gain).astype(jnp.bfloat16)


def vocab_logits(normed, rows):
    return lax.dot_general(
        normed, rows, (((1,), (1,)), ((), ())), preferred_element_type=jnp.float32
    )


def picked_logit(logits, offset, wanted):
    columns = offset + jnp.arange(logits.shape[1], dtype=jnp.int32)
    hits = columns[None, :] == wanted[:, None]
    return jnp.sum(jnp.where(hits, logits, 0.0), 1)


def body(
    queries,
    keys,
    values,
    key_position,
    compress_keys,
    compress_values,
    out_proj,
    residual,
    norm_gain,
    lm_head,
    targets,
    lengths,
):
    seq_count = lax.axis_size("seq")
    seq_pos = lax.axis_index("seq")
    batch_count = lax.axis_size("batch")
    batch_pos = lax.axis_index("batch")
    qcount = queries.shape[1]
    skip = keys.shape[1] // qcount
    scored = targets.shape[1]
    following = from_behind((keys[0, :STRIDE], values[0, :STRIDE]), "seq", -1)
    comp_keys = compress_rows(keys[0], following[0], key_position, compress_keys)
    comp_values = compress_rows(values[0], following[1], key_position, compress_values)
    every = lax.all_gather(jnp.stack([comp_keys, comp_values], 0), "seq", axis=1, tiled=True)
    heads = keys.shape[2] // HEAD_DIM
    blocks = every.shape[1]
    all_keys = every[0].reshape(blocks, heads, HEAD_DIM)
    all_values = every[1].reshape(blocks, heads, HEAD_DIM)
    group = queries.shape[2] // HEAD_DIM // heads
    query = queries[0].reshape(qcount, heads, group, HEAD_DIM)
    scores = jnp.einsum("qhgd,bhd->qhgb", query, all_keys, preferred_element_type=jnp.float32) * (
        1.0 / math.sqrt(HEAD_DIM)
    )
    index = seq_pos * qcount + jnp.arange(qcount, dtype=jnp.int32)
    limit = index * skip // STRIDE
    visible = (jnp.arange(blocks, dtype=jnp.int32)[None, :] <= limit[:, None])[:, None, None, :]
    scores = jnp.where(visible, scores, -1e30)
    peak = jnp.max(scores, -1, keepdims=True)
    weights = jnp.where(visible, jnp.exp(scores - peak), 0.0)
    probs = (weights / jnp.sum(weights, -1, keepdims=True)).astype(jnp.bfloat16)
    attended = jnp.einsum("qhgb,bhd->qhgd", probs, all_values, preferred_element_type=jnp.float32)
    attended = attended.astype(jnp.bfloat16).reshape(qcount, heads * group * HEAD_DIM)
    spots = jnp.arange(scored, dtype=jnp.int32) * skip + BLOCK - 1
    valid = (spots[None, :] < lengths[:, None]).astype(jnp.float32)
    count = jnp.sum(valid)
    width = out_proj.shape[1]
    rows_all = lax.all_gather(attended, ("seq", "batch"), axis=0, tiled=True)
    part = jnp.dot(rows_all, out_proj, preferred_element_type=jnp.float32)
    summed = lax.psum(part, "mp")
    local_res = (
        residual.reshape(batch_count, seq_count, qcount, width)
        .transpose(1, 0, 2, 3)
        .reshape(-1, width)
    )
    hidden = (local_res.astype(jnp.float32) + summed).astype(jnp.bfloat16)
    whole = lax.all_gather(hidden, "seq", axis=1, tiled=True)
    normed = normalize(whole, norm_gain)
    logits = vocab_logits(normed, lm_head)
    wanted = targets.reshape(batch_count, seq_count, qcount).transpose(1, 0, 2).reshape(-1)
    offset = lax.axis_index(("seq", "mp", "batch")) * lm_head.shape[0]
    picked = picked_logit(logits, offset, wanted)
    local_top = jnp.max(logits, 1)
    top = lax.pmax(local_top, ("seq", "mp", "batch"))
    local_sum = jnp.sum(jnp.exp(logits - top[:, None]), 1)
    total, target_logit = lax.psum((local_sum, picked), ("seq", "mp", "batch"))
    logprob = target_logit - (top + jnp.log(total))
    cube = logprob.reshape(seq_count, batch_count, qcount)
    token_logprob = cube[seq_pos, batch_pos][None, :]
    by_rollout = cube.transpose(1, 0, 2).reshape(batch_count, scored)
    sums = jnp.sum(valid * by_rollout, 1) / count
    rollout_score = sums[batch_pos][None]
    return (token_logprob, rollout_score)


def solution(mesh):
    in_specs = (
        P("batch", "seq", "mp"),
        P("batch", "seq", "mp"),
        P("batch", "seq", "mp"),
        P(),
        P(),
        P(),
        P("mp", "seq"),
        P(None, None, "seq"),
        P(),
        P(("seq", "mp", "batch"), None),
        P(),
        P(),
    )
    out_specs = (P("batch", "seq"), P("batch"))
    return jax.shard_map(body, mesh=mesh, in_specs=in_specs, out_specs=out_specs, check_vma=False)
```

profile of v0, /device:TPU:0, one launch (start us, length us, event | category | flops | bytes accessed | tf_op | source)
XLA Modules:
  0.0 194.4 jit_solution(1485913314387452292)
XLA Ops:
  7.2 0.9 slice_bitcast_fusion.1
  8.1 1.4 collective-permute-start
  9.5 1.3 slice_bitcast_fusion
  10.8 1.3 collective-permute-start.1
  12.1 0.6 iota_compare_fusion
  12.7 0.6 multiply_add_fusion
  13.3 0.9 slice.32
  14.3 0.9 slice.36
  15.2 0.7 copy.47
  16.0 1.3 reshape_squeeze.11
  17.3 0.9 pad_maximum_fusion.1
  18.3 1.6 fusion.6
  19.9 0.9 pad_maximum_fusion
  21.0 1.0 fusion.7
  22.1 2.6 %all_gather.9 = bf16[2,32,256]{2,1,0:T(8,128)(2,1)S(1)} all-gather(bf16[2,16,256]{2,1,0:T(8,128)(2,1)S(1)} %pad_maximum_fusion.2), channel_id=1, replica_groups=mesh['seq'=2,'mp'=4,'batch'=4] {'seq'}, dimensions={1}, use_global_device_ids=true | all-gather | bytes 49152 | tf_op jit(solution)/shard_map/all_gather | solution.py:76
  24.7 0.8 fusion.5
  25.5 0.8 fusion.32
  26.4 0.9 fusion.8
  27.3 25.7 %all-gather = bf16[8,4,1024]{2,1,0:T(4,128)(2,1)S(1)} all-gather(bf16[1,4,1024]{2,1,0:T(4,128)(2,1)S(1)} %reshape.113), channel_id=1, replica_groups=mesh['seq'=2,'mp'=4,'batch'=4] {'seq','batch'}, dimensions={0}, use_global_device_ids=true | all-gather | bytes 73728 | tf_op jit(solution)/shard_map/all_gather | solution.py:99
  53.0 3.7 %fusion.34 = f32[32,2048]{1,0:T(8,128)} fusion(bf16[32,1024]{1,0:T(8,128)(2,1)S(1)} %reshape.114, bf16[1024,2048]{1,0:T(8,128)(2,1)} %param.18), kind=kOutput, calls=%fused_computation.65 | convolution fusion | flops 134217728 | bytes 4521984 | tf_op jit(solution)/shard_map/dot_general | solution.py:100
  57.2 0.7 convert_reduce_fusion
  57.9 43.1 %all-reduce.3.cloned.1.call-done = f32[32,2048]{1,0:T(8,128)} async-done(((f32[32,2048]{1,0:T(8,128)}), f32[32,2048]{1,0:T(8,128)}) %all-reduce.3.cloned.1.call-update) | async-done | bytes 262160 | tf_op jit(solution)/shard_map/psum | solution.py:101
  101.0 1.0 add_convert_fusion.4
  102.0 2.0 %all_gather.11 = bf16[32,4096]{1,0:T(8,128)(2,1)S(1)} all-gather(bf16[32,2048]{1,0:T(8,128)(2,1)S(1)} %add_convert_fusion.4), channel_id=1, replica_groups=mesh['seq'=2,'mp'=4,'batch'=4] {'seq'}, dimensions={1}, use_global_device_ids=true | all-gather | bytes 393216 | tf_op jit(solution)/shard_map/all_gather | solution.py:108
  104.2 0.8 fusion.33
  105.0 39.3 %pmax.7 = f32[32]{0:T(128)S(1)} all-reduce(f32[32]{0:T(128)S(1)} %get-tuple-element.8), channel_id=1, replica_groups=mesh['seq'=2,'mp'=4,'batch'=4] {'seq','mp','batch'}, use_global_device_ids=true, to_apply=%region_7.8 | all-reduce | flops 32 | bytes 256 | tf_op jit(solution)/shard_map/pmax | solution.py:115
  144.3 0.2 exponential_reduce_fusion
  144.5 41.0 %all-reduce = (f32[32]{0:T(128)S(1)}, f32[32]{0:T(128)S(1)}) all-reduce(f32[32]{0:T(128)S(1)} %get-tuple-element.3, f32[32]{0:T(128)S(1)} %get-tuple-element.2), channel_id=1, replica_groups=mesh['seq'=2,'mp'=4,'batch'=4] {'seq','mp','batch'}, use_global_device_ids=true, to_apply=%region_5.6 | all-reduce | flops 64 | bytes 512 | tf_op jit(solution)/shard_map/psum | solution.py:117
  185.6 0.2 fusion.28
  185.8 0.7 broadcast_divide_fusion
  186.4 0.6 dynamic_slice.7
  187.0 0.5 dynamic-slice_bitcast_fusion
  (47 shorter events, 1.1 us)
Async XLA Ops:
  7.2 97.0 %copy-start = (bf16[256,4096]{1,0:T(8,128)(2,1)S(1)}, bf16[256,4096]{1,0:T(8,128)(2,1)}, u32[]{:S(2)}) copy-start(bf16[256,4096]{1,0:T(8,128)(2,1)} %param.21) | copy-start | bytes 6291460
  7.2 13.8 %copy-start.1 = (bf16[4096,128]{1,0:T(8,128)(2,1)S(1)}, bf16[4096,128]{1,0:T(8,128)(2,1)}, u32[]{:S(2)}) copy-start(bf16[4096,128]{1,0:T(8,128)(2,1)} %param.17) | copy-start | bytes 3145732
  7.2 93.8 %all-reduce.3.cloned.1.call-start = ((), (), s32[]{:S(2)}) async-start(), calls=%async_computation | async-start | bytes 524288 | tf_op jit(solution)/shard_map/psum | solution.py:101
  8.1 9.1 %collective-permute-start = (bf16[16,256]{1,0:T(8,128)(2,1)S(1)}, bf16[16,256]{1,0:T(8,128)(2,1)S(1)}, u32[]{:S(2)}, u32[]{:S(2)}) collective-permute-start(bf16[16,256]{1,0:T(8,128)(2,1)S(1)} %slice_bitcast_fusion.1), channel_id=1, source_target_pairs={{16,0},{17,1},{18,2},{19,3},{20,4},{21,5},{22,6},{23,7},{24,8},{25... | collective-permute-start | bytes 24584 | tf_op jit(solution)/shard_map/ppermute | solution.py:15
  10.8 9.1 %collective-permute-start.1 = (bf16[16,256]{1,0:T(8,128)(2,1)}, bf16[16,256]{1,0:T(8,128)(2,1)S(1)}, u32[]{:S(2)}, u32[]{:S(2)}) collective-permute-start(bf16[16,256]{1,0:T(8,128)(2,1)} %slice_bitcast_fusion), channel_id=1, source_target_pairs={{16,0},{17,1},{18,2},{19,3},{20,4},{21,5},{22,6},{23,7},{24,8},{25... | collective-permute-start | bytes 24584 | tf_op jit(solution)/shard_map/ppermute | solution.py:15
  20.9 35.9 %copy-start.2 = (bf16[4,8,2048]{2,1,0:T(8,128)(2,1)S(1)}, bf16[4,8,2048]{2,1,0:T(8,128)(2,1)}, u32[]{:S(2)}) copy-start(bf16[4,8,2048]{2,1,0:T(8,128)(2,1)} %param.19) | copy-start | bytes 393220
  21.0 36.0 %copy-start.4 = (s32[4,8]{1,0:T(4,128)S(1)}, s32[4,8]{1,0:T(4,128)}, u32[]{:S(2)}) copy-start(s32[4,8]{1,0:T(4,128)} %param.22) | copy-start | bytes 388
  21.0 36.2 %copy-start.6 = (s32[4]{0:T(128)S(1)}, s32[4]{0:T(128)}, u32[]{:S(2)}) copy-start(s32[4]{0:T(128)} %param.23) | copy-start | bytes 52
  22.0 82.1 %copy-start.3 = (f32[4096]{0:T(1024)S(1)}, f32[4096]{0:T(1024)}, u32[]{:S(2)}) copy-start(f32[4096]{0:T(1024)} %param.20) | copy-start | bytes 49156
  53.0 132.6 %copy-start.5 = (s32[2,4]{1,0:T(2,128)S(1)}, s32[2,4]{1,0:T(2,128)}, u32[]{:S(2)}) copy-start(s32[2,4]{1,0:T(2,128)} %multiply_add_fusion) | copy-start | bytes 100
Sparse Core Ops, SparseCore 0:
  56.9 44.0 all-reduce.2
where the time goes:
time: 195 us; the launch traced here: 194 us
  blocking collectives  111 us (57%)
  waiting for transfers between devices  43.1 us (22%)
  between operations  14.3 us (7%)
  matrix products  8.86 us (5%)
  local copies, waits for them, and re-layouts  8.01 us (4%)
  other arithmetic  6.72 us (3%)
  starting transfers between devices  2.73 us (1%)
    psum x1, waiting for transfers between devices, body(): summed = lax.psum(part, 'mp')  43.1 us
    psum x1, blocking collectives, body(): total, target_logit = lax.psum((local_sum, picked), ('seq', 'mp', 'batch'))  41 us
    pmax x1, blocking collectives, body(): top = lax.pmax(local_top, ('seq', 'mp', 'batch'))  39.3 us
    all_gather x1, blocking collectives, body(): rows_all = lax.all_gather(attended, ('seq', 'batch'), axis=0, tiled=True)  25.7 us
  transfers between devices with their start and end apart: 3, of which 1 were waited for; matrix products, arithmetic and copies ran while one was open for 5% of the time, Pallas kernels for 0%

commit v1 on v0

--- a/solution.py
+++ b/solution.py
@@ -1,3 +1,4 @@
+import functools
 import math
 import jax
 import jax.numpy as jnp
@@ -7,6 +8,22 @@
 HEAD_DIM = 128
 BLOCK = 32
 STRIDE = 16
+
+
+def _deliver_cycles(patch, mesh_ax):
+    opened = lax.axis_size(mesh_ax)
+    all_rows, right_arr = (opened, lax.axis_index(mesh_ax))
+    local_now, ready = (patch, 1)
+    while ready < all_rows:
+        outer = lax.ppermute(local_now, mesh_ax, [(w, w ^ ready) for w in range(all_rows)])
+        earlier = jnp.concatenate([local_now, outer], axis=0)
+        clean = jnp.concatenate([outer, local_now], axis=0)
+        local_now = jnp.where(right_arr & ready == 0, earlier, clean)
+        ready = 2 * ready
+    return local_now
+
+
+roads_process = functools.partial(_deliver_cycles, mesh_ax=("seq", "batch"))
 
 
 def from_behind(block, axis, distance):
@@ -96,7 +113,7 @@
     valid = (spots[None, :] < lengths[:, None]).astype(jnp.float32)
     count = jnp.sum(valid)
     width = out_proj.shape[1]
-    rows_all = lax.all_gather(attended, ("seq", "batch"), axis=0, tiled=True)
+    rows_all = roads_process(attended)
     part = jnp.dot(rows_all, out_proj, preferred_element_type=jnp.float32)
     summed = lax.psum(part, "mp")
     local_res = (

time: 195 us -> 180 us (0.923)
  blocking collectives: 111 us -> 84.9 us
  starting transfers between devices: 2.73 us -> 9.02 us
  waiting for transfers between devices: 43.1 us -> 48.3 us
    all_gather x1 -> x0, blocking collectives: 25.7 us -> none  [body(): rows_all = lax.all_gather(attended, ('seq', 'batch'), axis=0, tiled=True)]
    ppermute x0 -> x3, starting transfers between devices: none -> 6.29 us  [_deliver_cycles(): lax.ppermute(local_now, mesh_ax, [(w, w ^ ready) for w in range(all_rows)])]
    ppermute x0 -> x3, waiting for transfers between devices: none -> 4.53 us  [_deliver_cycles(): lax.ppermute(local_now, mesh_ax, [(w, w ^ ready) for w in range(all_rows)])]
  transfers between devices with their start and end apart: 3 -> 6, of which waited for: 1 -> 4; matrix products, arithmetic and copies ran while one was open for 5% -> 5% of each run, Pallas kernels for 0% -> 0%
where the time goes in v1:
time: 180 us
  blocking collectives  84.9 us (47%)
  waiting for transfers between devices  48.3 us (27%)
  between operations  14.3 us (8%)
  starting transfers between devices  9.02 us (5%)
  matrix products  8.86 us (5%)
  local copies, waits for them, and re-layouts  7.98 us (4%)
  other arithmetic  6.16 us (3%)
    psum x1, waiting for transfers between devices, body(): summed = lax.psum(part, 'mp')  43.8 us
    psum x1, blocking collectives, body(): total, target_logit = lax.psum((local_sum, picked), ('seq', 'mp', 'batch'))  41 us
    pmax x1, blocking collectives, body(): top = lax.pmax(local_top, ('seq', 'mp', 'batch'))  39.3 us
    ppermute x3, starting transfers between devices, _deliver_cycles(): lax.ppermute(local_now, mesh_ax, [(w, w ^ ready) for w in range(all_rows)])  6.29 us
    ppermute x3, waiting for transfers between devices, _deliver_cycles(): lax.ppermute(local_now, mesh_ax, [(w, w ^ ready) for w in range(all_rows)])  4.53 us
    dot_general x1, matrix products, body(): part = jnp.dot(rows_all, out_proj, preferred_element_type=jnp.float32)  3.72 us
  transfers between devices with their start and end apart: 6, of which 4 were waited for; matrix products, arithmetic and copies ran while one was open for 5% of the time, Pallas kernels for 0%

profile of v1, /device:TPU:0, one launch (start us, length us, event | category | flops | bytes accessed | tf_op | source)
XLA Modules:
  0.0 179.6 jit_solution(5402693705473911101)
XLA Ops:
  7.2 0.9 slice_bitcast_fusion.1
  8.1 1.4 collective-permute-start
  9.5 1.3 slice_bitcast_fusion
  10.8 1.3 collective-permute-start.1
  12.1 0.6 iota_compare_fusion
  12.7 0.9 slice.32
  13.7 0.9 slice.36
  14.6 0.7 copy.35
  15.4 1.3 reshape_squeeze.11
  16.7 0.9 pad_maximum_fusion.1
  17.7 1.6 fusion.6
  19.3 0.9 pad_maximum_fusion
  20.4 1.0 fusion.7
  21.5 2.6 %all_gather.6 = bf16[2,32,256]{2,1,0:T(8,128)(2,1)S(1)} all-gather(bf16[2,16,256]{2,1,0:T(8,128)(2,1)S(1)} %pad_maximum_fusion.2), channel_id=1, replica_groups=mesh['seq'=2,'mp'=4,'batch'=4] {'seq'}, dimensions={1}, use_global_device_ids=true | all-gather | bytes 49152 | tf_op jit(solution)/shard_map/all_gather | solution.py:93
  24.1 0.8 fusion.5
  24.9 0.8 fusion.40
  25.8 0.9 fusion.8
  26.7 3.1 %collective-permute-start.2 = (bf16[4,1024]{1,0:T(4,128)(2,1)S(1)}, bf16[4,1024]{1,0:T(4,128)(2,1)S(1)}, u32[]{:S(2)}, u32[]{:S(2)}) collective-permute-start(bf16[4,1024]{1,0:T(4,128)(2,1)S(1)} %reshape.109), channel_id=1, source_target_pairs={{0,1},{1,0},{2,3},{3,2},{16,17},{17,16},{18,19},{19,18},{4,5},{5,4... | collective-permute-start | bytes 24584 | tf_op jit(solution)/shard_map/ppermute | solution.py:18
  29.8 1.6 collective-permute-done.2
  31.4 3.1 %collective-permute-start.3 = (bf16[8,1024]{1,0:T(8,128)(2,1)S(1)}, bf16[8,1024]{1,0:T(8,128)(2,1)S(1)}, u32[]{:S(2)}, u32[]{:S(2)}) collective-permute-start(bf16[8,1024]{1,0:T(8,128)(2,1)S(1)} %maximum_select_fusion.3), channel_id=1, source_target_pairs={{0,2},{1,3},{2,0},{3,1},{16,18},{17,19},{18,16},{19,17},{4,6},{5,7... | collective-permute-start | bytes 49160 | tf_op jit(solution)/shard_map/ppermute | solution.py:18
  34.5 1.7 collective-permute-done.3
  36.4 1.2 collective-permute-done.4
  37.5 3.7 %fusion.24 = f32[32,2048]{1,0:T(8,128)} fusion(bf16[1024,2048]{1,0:T(8,128)(2,1)} %param.18, bf16[16,1024]{1,0:T(8,128)(2,1)S(1)} %collective-permute-done.4, bf16[16,1024]{1,0:T(8,128)(2,1)S(1)} %maximum_select_fusion.2, pred[]{:T(512)S(6)} %eq.28), kind=kOutput, calls=%fused_computation.36 | convolution fusion | flops 134512640 | bytes 4521985 | tf_op jit(solution)/shard_map/dot_general | solution.py:117
  41.7 0.7 convert_reduce_fusion
  42.4 43.8 %all-reduce.3.cloned.1.call-done = f32[32,2048]{1,0:T(8,128)} async-done(((f32[32,2048]{1,0:T(8,128)}), f32[32,2048]{1,0:T(8,128)}) %all-reduce.3.cloned.1.call-update) | async-done | bytes 262160 | tf_op jit(solution)/shard_map/psum | solution.py:118
  86.2 1.0 add_convert_fusion.4
  87.2 2.0 %all_gather.7 = bf16[32,4096]{1,0:T(8,128)(2,1)S(1)} all-gather(bf16[32,2048]{1,0:T(8,128)(2,1)S(1)} %add_convert_fusion.4), channel_id=1, replica_groups=mesh['seq'=2,'mp'=4,'batch'=4] {'seq'}, dimensions={1}, use_global_device_ids=true | all-gather | bytes 393216 | tf_op jit(solution)/shard_map/all_gather | solution.py:125
  89.3 0.8 fusion.41
  90.2 39.3 %pmax.7 = f32[32]{0:T(128)S(1)} all-reduce(f32[32]{0:T(128)S(1)} %get-tuple-element.8), channel_id=1, replica_groups=mesh['seq'=2,'mp'=4,'batch'=4] {'seq','mp','batch'}, use_global_device_ids=true, to_apply=%region_7.8 | all-reduce | flops 32 | bytes 256 | tf_op jit(solution)/shard_map/pmax | solution.py:132
  129.7 41.0 %all-reduce = (f32[32]{0:T(128)S(1)}, f32[32]{0:T(128)S(1)}) all-reduce(f32[32]{0:T(128)S(1)} %get-tuple-element.3, f32[32]{0:T(128)S(1)} %get-tuple-element.2), channel_id=1, replica_groups=mesh['seq'=2,'mp'=4,'batch'=4] {'seq','mp','batch'}, use_global_device_ids=true, to_apply=%region_5.6 | all-reduce | flops 64 | bytes 512 | tf_op jit(solution)/shard_map/psum | solution.py:134
  170.9 0.7 broadcast_divide_fusion
  171.6 0.6 dynamic_slice.7
  (51 shorter events, 2.1 us)
Async XLA Ops:
  7.2 82.2 %copy-start = (bf16[256,4096]{1,0:T(8,128)(2,1)S(1)}, bf16[256,4096]{1,0:T(8,128)(2,1)}, u32[]{:S(2)}) copy-start(bf16[256,4096]{1,0:T(8,128)(2,1)} %param.21) | copy-start | bytes 6291460
  7.2 13.2 %copy-start.1 = (bf16[4096,128]{1,0:T(8,128)(2,1)S(1)}, bf16[4096,128]{1,0:T(8,128)(2,1)}, u32[]{:S(2)}) copy-start(bf16[4096,128]{1,0:T(8,128)(2,1)} %param.17) | copy-start | bytes 3145732
  7.2 79.0 %all-reduce.3.cloned.1.call-start = ((), (), s32[]{:S(2)}) async-start(), calls=%async_computation | async-start | bytes 524288 | tf_op jit(solution)/shard_map/psum | solution.py:118
  8.1 8.5 %collective-permute-start = (bf16[16,256]{1,0:T(8,128)(2,1)S(1)}, bf16[16,256]{1,0:T(8,128)(2,1)S(1)}, u32[]{:S(2)}, u32[]{:S(2)}) collective-permute-start(bf16[16,256]{1,0:T(8,128)(2,1)S(1)} %slice_bitcast_fusion.1), channel_id=1, source_target_pairs={{16,0},{17,1},{18,2},{19,3},{20,4},{21,5},{22,6},{23,7},{24,8},{25... | collective-permute-start | bytes 24584 | tf_op jit(solution)/shard_map/ppermute | solution.py:32
  10.8 8.5 %collective-permute-start.1 = (bf16[16,256]{1,0:T(8,128)(2,1)}, bf16[16,256]{1,0:T(8,128)(2,1)S(1)}, u32[]{:S(2)}, u32[]{:S(2)}) collective-permute-start(bf16[16,256]{1,0:T(8,128)(2,1)} %slice_bitcast_fusion), channel_id=1, source_target_pairs={{16,0},{17,1},{18,2},{19,3},{20,4},{21,5},{22,6},{23,7},{24,8},{25... | collective-permute-start | bytes 24584 | tf_op jit(solution)/shard_map/ppermute | solution.py:32
  20.3 21.0 %copy-start.2 = (bf16[4,8,2048]{2,1,0:T(8,128)(2,1)S(1)}, bf16[4,8,2048]{2,1,0:T(8,128)(2,1)}, u32[]{:S(2)}) copy-start(bf16[4,8,2048]{2,1,0:T(8,128)(2,1)} %param.19) | copy-start | bytes 393220
  20.4 21.2 %copy-start.4 = (s32[4,8]{1,0:T(4,128)S(1)}, s32[4,8]{1,0:T(4,128)}, u32[]{:S(2)}) copy-start(s32[4,8]{1,0:T(4,128)} %param.22) | copy-start | bytes 388
  20.4 21.3 %copy-start.5 = (s32[4]{0:T(128)S(1)}, s32[4]{0:T(128)}, u32[]{:S(2)}) copy-start(s32[4]{0:T(128)} %param.23) | copy-start | bytes 52
  21.4 67.9 %copy-start.3 = (f32[4096]{0:T(1024)S(1)}, f32[4096]{0:T(1024)}, u32[]{:S(2)}) copy-start(f32[4096]{0:T(1024)} %param.20) | copy-start | bytes 49156
  26.7 4.7 %collective-permute-start.2 = (bf16[4,1024]{1,0:T(4,128)(2,1)S(1)}, bf16[4,1024]{1,0:T(4,128)(2,1)S(1)}, u32[]{:S(2)}, u32[]{:S(2)}) collective-permute-start(bf16[4,1024]{1,0:T(4,128)(2,1)S(1)} %reshape.109), channel_id=1, source_target_pairs={{0,1},{1,0},{2,3},{3,2},{16,17},{17,16},{18,19},{19,18},{4,5},{5,4... | collective-permute-start | bytes 24584 | tf_op jit(solution)/shard_map/ppermute | solution.py:18
  31.4 4.8 %collective-permute-start.3 = (bf16[8,1024]{1,0:T(8,128)(2,1)S(1)}, bf16[8,1024]{1,0:T(8,128)(2,1)S(1)}, u32[]{:S(2)}, u32[]{:S(2)}) collective-permute-start(bf16[8,1024]{1,0:T(8,128)(2,1)S(1)} %maximum_select_fusion.3), channel_id=1, source_target_pairs={{0,2},{1,3},{2,0},{3,1},{16,18},{17,19},{18,16},{19,17},{4,6},{5,7... | collective-permute-start | bytes 49160 | tf_op jit(solution)/shard_map/ppermute | solution.py:18
  36.3 1.3 collective-permute-start.4
Sparse Core Ops, SparseCore 0:
  41.4 44.7 all-reduce.2
